TPU v7x, 128 devices: a whole 4x4x4 slice. The times are simulated.
128 devices in a mesh: hst: 2 (over core), row: 4 (over x), col: 16 (over z, y).
Axes of the slice: x: 4, y: 4, z: 4, core: 2. Of those that a mesh axis runs over, the one named last changes fastest.
Arguments:
- tables: bfloat16 [1024, 1024, 128], P(('hst', 'row', 'col')), may hold values from -6 to 6
- indices: int32 [1024, 2048, 4], P(('hst', 'row', 'col')), may hold values from 0 to 1023
- lengths: int32 [1024, 2048], P(('hst', 'row', 'col')), may hold values from 1 to 4, as said below
- table_slot: int32 [1024], replicated, may hold values from 0 to 1023, each once
- dense_feature: bfloat16 [2048, 128], P(('hst', 'row', 'col')), may hold values from -48 to 48
- left_proj: bfloat16 [128, 1025], replicated, may hold values from -0.1875 to 0.1875
- right_proj: bfloat16 [128, 1025], replicated, may hold values from -0.1875 to 0.1875
Outputs:
- interaction: bfloat16 [2048, 16384], P(('hst', 'row', 'col'))
Inputs may be any that keep to these rules, and one draw needn't show every extreme that they name: Each bag uses its first lengths ids; some bag holds 4 ids.
All inputs are finite; a program needn't handle non-finite values.
Results may differ from a plain program's by a relative error of at most 0.0063.
Values may be sent and summed in bfloat16 or wider, within the bound.
A program may use at most 64 MiB of HBM per device.

v0:
```python
import jax
import jax.numpy as jnp
from jax import lax
from jax.sharding import PartitionSpec as P


def pool_table(table, row_ids, bag_lens, bag_size):
    all_samples = row_ids.shape[0]
    table_rows = table.shape[0]
    feature_width = table.shape[1]
    block = 512
    row_iota = lax.broadcasted_iota(jnp.int32, (1, table_rows), 1)

    def one_block(items):
        block_ids, block_lens = items

        def add_ids(position, counts):
            chosen_ids = lax.dynamic_index_in_dim(block_ids, position, 1, keepdims=False)
            hit = (chosen_ids[:, None] == row_iota) & (position < block_lens)[:, None]
            return counts + hit.astype(jnp.bfloat16)

        counts = jnp.zeros((block, table_rows), jnp.bfloat16)
        counts = lax.fori_loop(0, bag_size, add_ids, counts)
        return jnp.dot(counts, table, preferred_element_type=jnp.float32).astype(jnp.bfloat16)

    grouped_ids = row_ids.reshape(all_samples // block, block, row_ids.shape[1])
    grouped_lens = bag_lens.reshape(all_samples // block, block)
    pooled = lax.map(one_block, (grouped_ids, grouped_lens))
    return pooled.reshape(all_samples, feature_width)


def shards(tables, indices, lengths, table_slot, dense_feature, left_proj, right_proj):
    tab_dev, all_samples, bag_size = indices.shape
    feature_width = tables.shape[2]
    devices = lax.axis_size(("hst", "row", "col"))
    own_samples = all_samples // devices
    proj_rows = left_proj.shape[0]
    tables_total = left_proj.shape[1] - 1
    pooled = lax.map(
        lambda items: pool_table(items[0], items[1], items[2], bag_size), (tables, indices, lengths)
    )
    blocks = pooled.reshape(tab_dev, devices, own_samples, feature_width)
    positions = jnp.arange(tables_total, dtype=jnp.int32)
    within = positions % tab_dev
    source = positions // tab_dev
    slot_here = source * tab_dev + within
    projections = jnp.concatenate([left_proj, right_proj], axis=0)
    selector = (table_slot[:, None] == slot_here[None, :]).astype(jnp.bfloat16)
    proj_here = jnp.dot(projections[:, 1:], selector, preferred_element_type=jnp.float32).astype(
        jnp.bfloat16
    )
    received = lax.all_to_all(
        blocks, ("hst", "row", "col"), split_axis=1, concat_axis=0, tiled=True
    )
    count = received.shape[2]
    flattened = received.reshape(tables_total, count * feature_width)
    mixed_all = jnp.dot(proj_here, flattened, preferred_element_type=jnp.float32)
    mixed_all = mixed_all.reshape(2 * proj_rows, count, feature_width)
    dense_column = projections[:, 0].astype(jnp.float32)
    mixed_all = mixed_all + dense_column[:, None, None] * dense_feature[None].astype(jnp.float32)
    mixed_all = mixed_all.astype(jnp.bfloat16)
    left_side = mixed_all[:proj_rows]
    right_side = mixed_all[proj_rows:]
    products = jnp.einsum("kbe,lbe->bkl", left_side, right_side, preferred_element_type=jnp.float32)
    products = products * (1.0 / feature_width)
    return products.reshape(own_samples, proj_rows * proj_rows).astype(jnp.bfloat16)


def solution(mesh):
    in_specs = (
        P(("hst", "row", "col"), None, None),
        P(("hst", "row", "col"), None, None),
        P(("hst", "row", "col"), None),
        P(),
        P(("hst", "row", "col"), None),
        P(),
        P(),
    )
    out_specs = P(("hst", "row", "col"), None)
    return jax.shard_map(shards, mesh=mesh, in_specs=in_specs, out_specs=out_specs, check_vma=False)
```

profile of v0, /device:TPU:1, one launch (start us, length us, event | category | flops | bytes accessed | tf_op | source)
XLA Modules:
  0.0 215.4 jit_solution(7283805805666844912)
XLA Ops:
  0.0 125.8 %while.38 = (s32[]{:T(128)}, bf16[8,2048,128]{2,1,0:T(8,128)(2,1)}, s32[8,2048,4]{1,2,0:T(4,128)}, s32[8,2048]{1,0:T(8,128)}, bf16[8,1024,128]{2,1,0:T(8,128)(2,...) while((s32[]{:T(128)}, bf16[8,2048,128]{2,1,0:T(8,128)(2,1)}, ...), condition=%wide.region_5.6_spmd, body=%wide.region_0.5_spmd.sunk | while | flops 138478080 | bytes 5248493 | solution.py:39
  2.6 12.3 %while.39 = (s32[]{:T(128)}, bf16[4,512,128]{2,1,0:T(8,128)(2,1)S(1)}, s32[4,512,4]{1,2,0:T(4,128)S(1)}, s32[4,512]{1,0:T(4,128)S(1)}, bf16[1024,128]{1,0:T(8,12...) while((s32[]{:T(128)}, bf16[4,512,128]{2,1,0:T(8,128)(2,1)S(1)}, ...), condition=%wide.region_4.4_spmd.clone, body=%wide.region_1.3_spmd.clone.sunk | while | flops 138478080 | bytes 3577112 | solution.py:28
  2.7 2.5 %while.40 = (s32[]{:T(128)}, bf16[512,1024]{1,0:T(8,128)(2,1)S(1)}, s32[512,4]{0,1:T(4,128)S(1)}, s32[1,1024]{1,0:T(1,128)S(1)}, s32[512]{0:T(512)S(1)}, /*index=5*/s32[]{:T(128)}, s32[]{:T(128)}) while((s32[]{:T(128)}, bf16[512,1024]{1,0:T(8,128)(2,1)S(1)}, s32[512,4]{0,1:T(4,128)S(1)}, s32[1,1024]{1,0:T(1,128)S(1)}, ...), condition=%wide.region_3.2_spmd.clone, body=%wide.region_2.1_spmd.clone.sunk | while | flops 4194819 | bytes 2110567 | solution.py:23
  5.8 2.5 %while.40 = (s32[]{:T(128)}, bf16[512,1024]{1,0:T(8,128)(2,1)S(1)}, s32[512,4]{0,1:T(4,128)S(1)}, s32[1,1024]{1,0:T(1,128)S(1)}, s32[512]{0:T(512)S(1)}, /*index=5*/s32[]{:T(128)}, s32[]{:T(128)}) while((s32[]{:T(128)}, bf16[512,1024]{1,0:T(8,128)(2,1)S(1)}, s32[512,4]{0,1:T(4,128)S(1)}, s32[1,1024]{1,0:T(1,128)S(1)}, ...), condition=%wide.region_3.2_spmd.clone, body=%wide.region_2.1_spmd.clone.sunk | while | flops 4194819 | bytes 2110567 | solution.py:23
  8.8 2.5 %while.40 = (s32[]{:T(128)}, bf16[512,1024]{1,0:T(8,128)(2,1)S(1)}, s32[512,4]{0,1:T(4,128)S(1)}, s32[1,1024]{1,0:T(1,128)S(1)}, s32[512]{0:T(512)S(1)}, /*index=5*/s32[]{:T(128)}, s32[]{:T(128)}) while((s32[]{:T(128)}, bf16[512,1024]{1,0:T(8,128)(2,1)S(1)}, s32[512,4]{0,1:T(4,128)S(1)}, s32[1,1024]{1,0:T(1,128)S(1)}, ...), condition=%wide.region_3.2_spmd.clone, body=%wide.region_2.1_spmd.clone.sunk | while | flops 4194819 | bytes 2110567 | solution.py:23
  11.9 2.5 %while.40 = (s32[]{:T(128)}, bf16[512,1024]{1,0:T(8,128)(2,1)S(1)}, s32[512,4]{0,1:T(4,128)S(1)}, s32[1,1024]{1,0:T(1,128)S(1)}, s32[512]{0:T(512)S(1)}, /*index=5*/s32[]{:T(128)}, s32[]{:T(128)}) while((s32[]{:T(128)}, bf16[512,1024]{1,0:T(8,128)(2,1)S(1)}, s32[512,4]{0,1:T(4,128)S(1)}, s32[1,1024]{1,0:T(1,128)S(1)}, ...), condition=%wide.region_3.2_spmd.clone, body=%wide.region_2.1_spmd.clone.sunk | while | flops 4194819 | bytes 2110567 | solution.py:23
  18.3 12.3 %while.39 = (s32[]{:T(128)}, bf16[4,512,128]{2,1,0:T(8,128)(2,1)S(1)}, s32[4,512,4]{1,2,0:T(4,128)S(1)}, s32[4,512]{1,0:T(4,128)S(1)}, bf16[1024,128]{1,0:T(8,12...) while((s32[]{:T(128)}, bf16[4,512,128]{2,1,0:T(8,128)(2,1)S(1)}, ...), condition=%wide.region_4.4_spmd.clone, body=%wide.region_1.3_spmd.clone.sunk | while | flops 138478080 | bytes 3577112 | solution.py:28
  18.4 2.5 %while.40 = (s32[]{:T(128)}, bf16[512,1024]{1,0:T(8,128)(2,1)S(1)}, s32[512,4]{0,1:T(4,128)S(1)}, s32[1,1024]{1,0:T(1,128)S(1)}, s32[512]{0:T(512)S(1)}, /*index=5*/s32[]{:T(128)}, s32[]{:T(128)}) while((s32[]{:T(128)}, bf16[512,1024]{1,0:T(8,128)(2,1)S(1)}, s32[512,4]{0,1:T(4,128)S(1)}, s32[1,1024]{1,0:T(1,128)S(1)}, ...), condition=%wide.region_3.2_spmd.clone, body=%wide.region_2.1_spmd.clone.sunk | while | flops 4194819 | bytes 2110567 | solution.py:23
  21.5 2.5 %while.40 = (s32[]{:T(128)}, bf16[512,1024]{1,0:T(8,128)(2,1)S(1)}, s32[512,4]{0,1:T(4,128)S(1)}, s32[1,1024]{1,0:T(1,128)S(1)}, s32[512]{0:T(512)S(1)}, /*index=5*/s32[]{:T(128)}, s32[]{:T(128)}) while((s32[]{:T(128)}, bf16[512,1024]{1,0:T(8,128)(2,1)S(1)}, s32[512,4]{0,1:T(4,128)S(1)}, s32[1,1024]{1,0:T(1,128)S(1)}, ...), condition=%wide.region_3.2_spmd.clone, body=%wide.region_2.1_spmd.clone.sunk | while | flops 4194819 | bytes 2110567 | solution.py:23
  27.6 2.5 %while.40 = (s32[]{:T(128)}, bf16[512,1024]{1,0:T(8,128)(2,1)S(1)}, s32[512,4]{0,1:T(4,128)S(1)}, s32[1,1024]{1,0:T(1,128)S(1)}, s32[512]{0:T(512)S(1)}, /*index=5*/s32[]{:T(128)}, s32[]{:T(128)}) while((s32[]{:T(128)}, bf16[512,1024]{1,0:T(8,128)(2,1)S(1)}, s32[512,4]{0,1:T(4,128)S(1)}, s32[1,1024]{1,0:T(1,128)S(1)}, ...), condition=%wide.region_3.2_spmd.clone, body=%wide.region_2.1_spmd.clone.sunk | while | flops 4194819 | bytes 2110567 | solution.py:23
  34.1 12.3 %while.39 = (s32[]{:T(128)}, bf16[4,512,128]{2,1,0:T(8,128)(2,1)S(1)}, s32[4,512,4]{1,2,0:T(4,128)S(1)}, s32[4,512]{1,0:T(4,128)S(1)}, bf16[1024,128]{1,0:T(8,12...) while((s32[]{:T(128)}, bf16[4,512,128]{2,1,0:T(8,128)(2,1)S(1)}, ...), condition=%wide.region_4.4_spmd.clone, body=%wide.region_1.3_spmd.clone.sunk | while | flops 138478080 | bytes 3577112 | solution.py:28
  37.2 2.5 %while.40 = (s32[]{:T(128)}, bf16[512,1024]{1,0:T(8,128)(2,1)S(1)}, s32[512,4]{0,1:T(4,128)S(1)}, s32[1,1024]{1,0:T(1,128)S(1)}, s32[512]{0:T(512)S(1)}, /*index=5*/s32[]{:T(128)}, s32[]{:T(128)}) while((s32[]{:T(128)}, bf16[512,1024]{1,0:T(8,128)(2,1)S(1)}, s32[512,4]{0,1:T(4,128)S(1)}, s32[1,1024]{1,0:T(1,128)S(1)}, ...), condition=%wide.region_3.2_spmd.clone, body=%wide.region_2.1_spmd.clone.sunk | while | flops 4194819 | bytes 2110567 | solution.py:23
  40.3 2.5 %while.40 = (s32[]{:T(128)}, bf16[512,1024]{1,0:T(8,128)(2,1)S(1)}, s32[512,4]{0,1:T(4,128)S(1)}, s32[1,1024]{1,0:T(1,128)S(1)}, s32[512]{0:T(512)S(1)}, /*index=5*/s32[]{:T(128)}, s32[]{:T(128)}) while((s32[]{:T(128)}, bf16[512,1024]{1,0:T(8,128)(2,1)S(1)}, s32[512,4]{0,1:T(4,128)S(1)}, s32[1,1024]{1,0:T(1,128)S(1)}, ...), condition=%wide.region_3.2_spmd.clone, body=%wide.region_2.1_spmd.clone.sunk | while | flops 4194819 | bytes 2110567 | solution.py:23
  43.3 2.5 %while.40 = (s32[]{:T(128)}, bf16[512,1024]{1,0:T(8,128)(2,1)S(1)}, s32[512,4]{0,1:T(4,128)S(1)}, s32[1,1024]{1,0:T(1,128)S(1)}, s32[512]{0:T(512)S(1)}, /*index=5*/s32[]{:T(128)}, s32[]{:T(128)}) while((s32[]{:T(128)}, bf16[512,1024]{1,0:T(8,128)(2,1)S(1)}, s32[512,4]{0,1:T(4,128)S(1)}, s32[1,1024]{1,0:T(1,128)S(1)}, ...), condition=%wide.region_3.2_spmd.clone, body=%wide.region_2.1_spmd.clone.sunk | while | flops 4194819 | bytes 2110567 | solution.py:23
  49.8 12.3 %while.39 = (s32[]{:T(128)}, bf16[4,512,128]{2,1,0:T(8,128)(2,1)S(1)}, s32[4,512,4]{1,2,0:T(4,128)S(1)}, s32[4,512]{1,0:T(4,128)S(1)}, bf16[1024,128]{1,0:T(8,12...) while((s32[]{:T(128)}, bf16[4,512,128]{2,1,0:T(8,128)(2,1)S(1)}, ...), condition=%wide.region_4.4_spmd.clone, body=%wide.region_1.3_spmd.clone.sunk | while | flops 138478080 | bytes 3577112 | solution.py:28
  49.9 2.5 %while.40 = (s32[]{:T(128)}, bf16[512,1024]{1,0:T(8,128)(2,1)S(1)}, s32[512,4]{0,1:T(4,128)S(1)}, s32[1,1024]{1,0:T(1,128)S(1)}, s32[512]{0:T(512)S(1)}, /*index=5*/s32[]{:T(128)}, s32[]{:T(128)}) while((s32[]{:T(128)}, bf16[512,1024]{1,0:T(8,128)(2,1)S(1)}, s32[512,4]{0,1:T(4,128)S(1)}, s32[1,1024]{1,0:T(1,128)S(1)}, ...), condition=%wide.region_3.2_spmd.clone, body=%wide.region_2.1_spmd.clone.sunk | while | flops 4194819 | bytes 2110567 | solution.py:23
  52.9 2.5 %while.40 = (s32[]{:T(128)}, bf16[512,1024]{1,0:T(8,128)(2,1)S(1)}, s32[512,4]{0,1:T(4,128)S(1)}, s32[1,1024]{1,0:T(1,128)S(1)}, s32[512]{0:T(512)S(1)}, /*index=5*/s32[]{:T(128)}, s32[]{:T(128)}) while((s32[]{:T(128)}, bf16[512,1024]{1,0:T(8,128)(2,1)S(1)}, s32[512,4]{0,1:T(4,128)S(1)}, s32[1,1024]{1,0:T(1,128)S(1)}, ...), condition=%wide.region_3.2_spmd.clone, body=%wide.region_2.1_spmd.clone.sunk | while | flops 4194819 | bytes 2110567 | solution.py:23
  56.0 2.5 %while.40 = (s32[]{:T(128)}, bf16[512,1024]{1,0:T(8,128)(2,1)S(1)}, s32[512,4]{0,1:T(4,128)S(1)}, s32[1,1024]{1,0:T(1,128)S(1)}, s32[512]{0:T(512)S(1)}, /*index=5*/s32[]{:T(128)}, s32[]{:T(128)}) while((s32[]{:T(128)}, bf16[512,1024]{1,0:T(8,128)(2,1)S(1)}, s32[512,4]{0,1:T(4,128)S(1)}, s32[1,1024]{1,0:T(1,128)S(1)}, ...), condition=%wide.region_3.2_spmd.clone, body=%wide.region_2.1_spmd.clone.sunk | while | flops 4194819 | bytes 2110567 | solution.py:23
  65.5 12.3 %while.39 = (s32[]{:T(128)}, bf16[4,512,128]{2,1,0:T(8,128)(2,1)S(1)}, s32[4,512,4]{1,2,0:T(4,128)S(1)}, s32[4,512]{1,0:T(4,128)S(1)}, bf16[1024,128]{1,0:T(8,12...) while((s32[]{:T(128)}, bf16[4,512,128]{2,1,0:T(8,128)(2,1)S(1)}, ...), condition=%wide.region_4.4_spmd.clone, body=%wide.region_1.3_spmd.clone.sunk | while | flops 138478080 | bytes 3577112 | solution.py:28
  68.7 2.5 %while.40 = (s32[]{:T(128)}, bf16[512,1024]{1,0:T(8,128)(2,1)S(1)}, s32[512,4]{0,1:T(4,128)S(1)}, s32[1,1024]{1,0:T(1,128)S(1)}, s32[512]{0:T(512)S(1)}, /*index=5*/s32[]{:T(128)}, s32[]{:T(128)}) while((s32[]{:T(128)}, bf16[512,1024]{1,0:T(8,128)(2,1)S(1)}, s32[512,4]{0,1:T(4,128)S(1)}, s32[1,1024]{1,0:T(1,128)S(1)}, ...), condition=%wide.region_3.2_spmd.clone, body=%wide.region_2.1_spmd.clone.sunk | while | flops 4194819 | bytes 2110567 | solution.py:23
  74.8 2.5 %while.40 = (s32[]{:T(128)}, bf16[512,1024]{1,0:T(8,128)(2,1)S(1)}, s32[512,4]{0,1:T(4,128)S(1)}, s32[1,1024]{1,0:T(1,128)S(1)}, s32[512]{0:T(512)S(1)}, /*index=5*/s32[]{:T(128)}, s32[]{:T(128)}) while((s32[]{:T(128)}, bf16[512,1024]{1,0:T(8,128)(2,1)S(1)}, s32[512,4]{0,1:T(4,128)S(1)}, s32[1,1024]{1,0:T(1,128)S(1)}, ...), condition=%wide.region_3.2_spmd.clone, body=%wide.region_2.1_spmd.clone.sunk | while | flops 4194819 | bytes 2110567 | solution.py:23
  81.3 12.3 %while.39 = (s32[]{:T(128)}, bf16[4,512,128]{2,1,0:T(8,128)(2,1)S(1)}, s32[4,512,4]{1,2,0:T(4,128)S(1)}, s32[4,512]{1,0:T(4,128)S(1)}, bf16[1024,128]{1,0:T(8,12...) while((s32[]{:T(128)}, bf16[4,512,128]{2,1,0:T(8,128)(2,1)S(1)}, ...), condition=%wide.region_4.4_spmd.clone, body=%wide.region_1.3_spmd.clone.sunk | while | flops 138478080 | bytes 3577112 | solution.py:28
  81.3 2.5 %while.40 = (s32[]{:T(128)}, bf16[512,1024]{1,0:T(8,128)(2,1)S(1)}, s32[512,4]{0,1:T(4,128)S(1)}, s32[1,1024]{1,0:T(1,128)S(1)}, s32[512]{0:T(512)S(1)}, /*index=5*/s32[]{:T(128)}, s32[]{:T(128)}) while((s32[]{:T(128)}, bf16[512,1024]{1,0:T(8,128)(2,1)S(1)}, s32[512,4]{0,1:T(4,128)S(1)}, s32[1,1024]{1,0:T(1,128)S(1)}, ...), condition=%wide.region_3.2_spmd.clone, body=%wide.region_2.1_spmd.clone.sunk | while | flops 4194819 | bytes 2110567 | solution.py:23
  84.4 2.5 %while.40 = (s32[]{:T(128)}, bf16[512,1024]{1,0:T(8,128)(2,1)S(1)}, s32[512,4]{0,1:T(4,128)S(1)}, s32[1,1024]{1,0:T(1,128)S(1)}, s32[512]{0:T(512)S(1)}, /*index=5*/s32[]{:T(128)}, s32[]{:T(128)}) while((s32[]{:T(128)}, bf16[512,1024]{1,0:T(8,128)(2,1)S(1)}, s32[512,4]{0,1:T(4,128)S(1)}, s32[1,1024]{1,0:T(1,128)S(1)}, ...), condition=%wide.region_3.2_spmd.clone, body=%wide.region_2.1_spmd.clone.sunk | while | flops 4194819 | bytes 2110567 | solution.py:23
  97.0 12.3 %while.39 = (s32[]{:T(128)}, bf16[4,512,128]{2,1,0:T(8,128)(2,1)S(1)}, s32[4,512,4]{1,2,0:T(4,128)S(1)}, s32[4,512]{1,0:T(4,128)S(1)}, bf16[1024,128]{1,0:T(8,12...) while((s32[]{:T(128)}, bf16[4,512,128]{2,1,0:T(8,128)(2,1)S(1)}, ...), condition=%wide.region_4.4_spmd.clone, body=%wide.region_1.3_spmd.clone.sunk | while | flops 138478080 | bytes 3577112 | solution.py:28
  112.7 12.3 %while.39 = (s32[]{:T(128)}, bf16[4,512,128]{2,1,0:T(8,128)(2,1)S(1)}, s32[4,512,4]{1,2,0:T(4,128)S(1)}, s32[4,512]{1,0:T(4,128)S(1)}, bf16[1024,128]{1,0:T(8,12...) while((s32[]{:T(128)}, bf16[4,512,128]{2,1,0:T(8,128)(2,1)S(1)}, ...), condition=%wide.region_4.4_spmd.clone, body=%wide.region_1.3_spmd.clone.sunk | while | flops 138478080 | bytes 3577112 | solution.py:28
  125.8 5.4 %copy.9 = bf16[8,128,16,128]{3,2,0,1:T(8,128)(2,1)} copy(bf16[8,128,16,128]{3,2,1,0:T(8,128)(2,1)} %bitcast.66) | data formatting | bytes 8388608 | tf_op jit(solution)/shard_map/reshape | solution.py:42
  131.2 11.9 %all-to-all-start = ((bf16[8,128,16,128]{3,2,0,1:T(8,128)(2,1)}), bf16[8,128,16,128]{3,2,0,1:T(8,128)(2,1)}, u32[]{:S(2)}, u32[]{:S(2)}) async-start(bf16[8,128,16,128]{3,2,0,1:T(8,128)(2,1)} %copy.9), calls=%async_computation | async-start | bytes 8388608 | tf_op jit(solution)/shard_map/all_to_all | solution.py:52
  143.4 53.3 %all-to-all-done = bf16[8,128,16,128]{3,2,0,1:T(8,128)(2,1)} async-done(((bf16[8,128,16,128]{3,2,0,1:T(8,128)(2,1)}), bf16[8,128,16,128]{3,2,0,1:T(8,128)(2,1)}, u32[]{:S(2)}, u32[]{:S(2)}) %all-to-all-start) | async-done | bytes 4194336 | tf_op jit(solution)/shard_map/all_to_all | solution.py:52
  196.7 6.3 %copy.15 = bf16[128,8,16,128]{3,1,2,0:T(8,128)(2,1)} copy(bf16[128,8,16,128]{3,2,1,0:T(8,128)(2,1)} %bitcast.18) | data formatting | bytes 8388608
  203.0 6.4 %copy.10 = bf16[2048,1024]{1,0:T(8,128)(2,1)} copy(bf16[2048,1024]{0,1:T(8,128)(2,1)} %bitcast.64) | data formatting | bytes 8388608 | tf_op jit(solution)/shard_map/dot_general | solution.py:57
  209.4 4.4 %add_convert_fusion = bf16[256,16,128]{2,0,1:T(8,128)(2,1)S(1)} fusion(bf16[16,128,1024]{2,1,0:T(8,128)(2,1)} %bitcast.67, f32[16,128]{1,0:T(8,128)S(1)} %convert_element_type.40, f32[256]{0:T(256)S(1)} %bitcast.70, s32[1024]{0:T(1024)S(1)} %fusion.29, s32[1024]{0:T(1024)S(1)} %copy-done.3, bf16[256,1025]{0,1:T(8,128)(2,1)S(1)} %constant_dynamic-update-slice_fusion), kind=kOutput, calls=%fused_computation.17 | convolution fusion | flops 1613496320 | bytes 5784576 | tf_op jit(solution)/shard_map/dot_general | solution.py:57
  (623 shorter events, 157.9 us)
Async XLA Ops:
  131.2 12.0 %copy-start.2 = (bf16[16,128]{1,0:T(8,128)(2,1)S(1)}, bf16[16,128]{1,0:T(8,128)(2,1)}, u32[]{:S(2)}) copy-start(bf16[16,128]{1,0:T(8,128)(2,1)} %param.17) | copy-start | bytes 12292
  131.2 12.0 %copy-start = (bf16[128,1025]{0,1:T(8,128)(2,1)S(1)}, bf16[128,1025]{0,1:T(8,128)(2,1)}, u32[]{:S(2)}) copy-start(bf16[128,1025]{0,1:T(8,128)(2,1)} %param.18) | copy-start | bytes 787204
  131.2 12.1 %copy-start.1 = (bf16[128,1025]{0,1:T(8,128)(2,1)S(1)}, bf16[128,1025]{0,1:T(8,128)(2,1)}, u32[]{:S(2)}) copy-start(bf16[128,1025]{0,1:T(8,128)(2,1)} %param.19) | copy-start | bytes 787204
  131.2 65.5 %all-to-all-start = ((bf16[8,128,16,128]{3,2,0,1:T(8,128)(2,1)}), bf16[8,128,16,128]{3,2,0,1:T(8,128)(2,1)}, u32[]{:S(2)}, u32[]{:S(2)}) async-start(bf16[8,128,16,128]{3,2,0,1:T(8,128)(2,1)} %copy.9), calls=%async_computation | async-start | bytes 8388608 | tf_op jit(solution)/shard_map/all_to_all | solution.py:52
  203.0 6.4 %copy-start.3 = (s32[1024]{0:T(1024)S(1)}, s32[1024]{0:T(1024)}, u32[]{:S(2)}) copy-start(s32[1024]{0:T(1024)} %param.16) | copy-start | bytes 12292
where the time goes:
time: 219 us; the launch traced here: 215 us
  other arithmetic  73.6 us (34%)
  waiting for transfers between devices  53.3 us (24%)
  local copies, waits for them, and re-layouts  48.8 us (22%)
  matrix products  20.5 us (9%)
  starting transfers between devices  11.9 us (5%)
  loops' own time  7.05 us (3%)
    add x128, other arithmetic, add_ids(): return counts + hit.astype(jnp.bfloat16)  72.8 us
    all_to_all x1, waiting for transfers between devices, shards(): lax.all_to_all(blocks, ('hst', 'row', 'col'), split_axis=1, concat_axis=0...  53.3 us
    dot_general x32, matrix products, one_block(): jnp.dot(counts, table, preferred_element_type=jnp.float32)  15.7 us
    dynamic_slice x16, local copies, waits for them, and re-layouts, shards(): lax.map(lambda items: pool_table(items[0], items[1], items[2], bag_size),...  13 us
    all_to_all x1, starting transfers between devices, shards(): lax.all_to_all(blocks, ('hst', 'row', 'col'), split_axis=1, concat_axis=0...  11.9 us
    squeeze x8, local copies, waits for them, and re-layouts, shards(): lax.map(lambda items: pool_table(items[0], items[1], items[2], bag_size),...  7.79 us
    unnamed x11, local copies, waits for them, and re-layouts  7.48 us
    dynamic_update_slice x8, local copies, waits for them, and re-layouts, shards(): lax.map(lambda items: pool_table(items[0], items[1], items[2], bag_size),...  6.71 us
  transfers between devices with their start and end apart: 1, of which 1 were waited for; matrix products, arithmetic and copies ran while one was open for 0% of the time, Pallas kernels for 0%

commit v1 on v0

v1 whole, which is shorter than its diff:
```python
import functools

import jax
import jax.numpy as jnp
import numpy as np
from jax import lax
from jax.experimental import pallas as pl
from jax.experimental.pallas import tpu as pltpu
from jax.sharding import PartitionSpec as P

AXES = ("hst", "row", "col")
MESH = pl.DeviceIdType.MESH
LINE = (0, 1, 2, 1)


def split_offset(offset):
    return offset // 64, offset // 16 % 4, offset // 4 % 4, offset % 4


def hops(offset):
    _, dx, dz, dy = split_offset(offset)
    return LINE[dx] + LINE[dz] + LINE[dy]


ORDER = [0] + sorted(range(1, 128), key=lambda offset: -hops(offset))


def place():
    col = lax.axis_index("col")
    return lax.axis_index("hst"), lax.axis_index("row"), col // 4, lax.rem(col, 4)


def partner(me, dh, dx, dz, dy):
    h, x, z, y = me
    return (
        lax.rem(h + dh, 2),
        lax.rem(x + dx, 4),
        lax.rem(z + dz, 4) * 4 + lax.rem(y + dy, 4),
    )


def greet(me, sem, offsets):
    for offset in offsets:
        pl.semaphore_signal(sem, 1, device_id=partner(me, *offset), device_id_type=MESH)


X_LINE = [(0, i, 0, 0) for i in (1, 2, 3)]
Z_LINE = [(0, 0, i, 0) for i in (1, 2, 3)]
Y_LINE = [(0, 0, 0, i) for i in (1, 2, 3)]
H_LINE = [(1, 0, 0, 0)]


def kernel(
    tables, ids, lens, slots, dense, left_t, right_t, steps, out,
    table_t, pooled, send, recv, proj, shifted, total, wide,
    send_sem, recv_sem, x_sem, y_sem, h_sem,
):
    me = place()
    h, x, z, y = me
    tab_dev, bag, samples = ids.shape
    rows = tables.shape[1]
    width = tables.shape[2]
    own = dense.shape[0]
    block = 256
    groups = recv_sem.shape[0]
    per_group = len(ORDER) // groups
    depth = per_group * tab_dev

    barrier = pltpu.get_barrier_semaphore()
    greet(me, barrier, X_LINE + Y_LINE + Z_LINE + H_LINE)

    for t in range(tab_dev):
        table_t[t] = tables[t].T

    iota = lax.broadcasted_iota(jnp.int32, (16, block), 0).astype(jnp.int16)

    def pool_block(blk, _):
        start = pl.multiple_of(blk * block, block)
        for t in range(tab_dev):
            length = lens[pl.ds(t, 1), pl.ds(start, block)]
            row_ids = []
            for j in range(bag):
                row = ids[t, pl.ds(j, 1), pl.ds(start, block)]
                row_ids.append(jnp.where(j < length, row, -1))
            weights = []
            for j in range(bag):
                weight = jnp.ones((1, block), jnp.float32)
                for other in range(j + 1, bag):
                    weight += (row_ids[other] == row_ids[j]).astype(jnp.float32)
                weights.append(jnp.broadcast_to(weight, (16, block)).astype(jnp.bfloat16))
            keys = [jnp.broadcast_to(row, (16, block)).astype(jnp.int16) for row in row_ids]
            result = jnp.zeros((width, block), jnp.float32)
            for chunk in range(rows // block):
                pieces = []
                for piece in range(block // 16):
                    here = iota + jnp.int16(chunk * block + piece * 16)
                    counts = jnp.zeros((16, block), jnp.bfloat16)
                    for j in reversed(range(bag)):
                        counts = jnp.where(keys[j] == here, weights[j], counts)
                    pieces.append(counts)
                result += jnp.dot(
                    table_t[t, :, pl.ds(chunk * block, block)],
                    jnp.concatenate(pieces, axis=0),
                    preferred_element_type=jnp.float32,
                )
            pooled[pl.ds(t, block, stride=tab_dev), :] = result.T
        for part in range(block // own):
            piece = pooled[pl.ds(part * own * tab_dev, own * tab_dev), :]
            send[blk * (block // own) + part] = piece.reshape(own, tab_dev, width).astype(jnp.bfloat16)
        return 0

    blocks = samples // block
    quarter = blocks // 4
    lax.fori_loop(0, quarter, pool_block, 0)
    pl.semaphore_wait(barrier, 10)
    greet(me, x_sem, X_LINE)
    lax.fori_loop(quarter, 2 * quarter, pool_block, 0)
    pl.semaphore_wait(x_sem, 3)
    greet(me, y_sem, Y_LINE)
    lax.fori_loop(2 * quarter, 3 * quarter, pool_block, 0)
    pl.semaphore_wait(y_sem, 3)
    greet(me, h_sem, H_LINE)
    lax.fori_loop(3 * quarter, blocks, pool_block, 0)
    pl.semaphore_wait(h_sem, 1)

    for step in range(1, len(ORDER)):
        to_h, to_x, to_c = partner(me, *split_offset(ORDER[step]))
        pltpu.make_async_remote_copy(
            src_ref=send.at[to_h * 64 + to_x * 16 + to_c],
            dst_ref=recv.at[:, pl.ds(step * tab_dev, tab_dev), :],
            send_sem=send_sem,
            recv_sem=recv_sem.at[step // per_group],
            device_id=(to_h, to_x, to_c),
            device_id_type=MESH,
        ).start()
    recv[:, 0:tab_dev, :] = send[h * 64 + x * 16 + z * 4 + y]

    kept = left_t.shape[1]
    from_h = lax.rem(h + 2 - steps[0:1, :], 2)
    from_x = lax.rem(x + 4 - steps[1:2, :], 4)
    from_z = lax.rem(z + 4 - steps[2:3, :], 4)
    from_y = lax.rem(y + 4 - steps[3:4, :], 4)
    slot_here = (from_h * 64 + from_x * 16 + from_z * 4 + from_y) * tab_dev + steps[4:5, :]
    slot_here = slot_here.astype(jnp.float32)
    count = slots.shape[1]
    slot_col = jnp.broadcast_to(slots[...].astype(jnp.float32), (8, count)).T[:, 0:1]
    selector = jnp.where(slot_col == slot_here, 1.0, 0.0).astype(jnp.bfloat16)
    firsts = []
    for side, source in enumerate((left_t, right_t)):
        shifted[0 : count + 1, :] = source[...].astype(jnp.float32)
        firsts.append(shifted[0:8, :].T[:, 0:1])
        moved = shifted[1 : count + 1, :].T.astype(jnp.bfloat16)
        proj[pl.ds(side * kept, kept), :] = jnp.dot(
            moved, selector, preferred_element_type=jnp.float32
        ).astype(jnp.bfloat16)
    first = jnp.concatenate(firsts, axis=0)
    for b in range(own):
        row = dense[b : b + 1, :].astype(jnp.float32)
        total[b // 2, :, pl.ds(b % 2 * width, width)] = first * row

    for group in range(groups):
        arrived = per_group - (1 if group == 0 else 0)
        area = send.at[pl.ds(0, arrived)]
        pltpu.make_async_copy(area, area, recv_sem.at[group]).wait()
        last = group == groups - 1
        part = proj[:, pl.ds(group * depth, depth)]
        for pair in range(own // 2):
            both = jnp.concatenate(
                [recv[2 * pair, pl.ds(group * depth, depth), :], recv[2 * pair + 1, pl.ds(group * depth, depth), :]],
                axis=1,
            )
            mixed = total[pair] + jnp.dot(part, both, preferred_element_type=jnp.float32)
            if not last:
                total[pair] = mixed
                continue
            mixed = mixed.astype(jnp.bfloat16)
            for side in range(2):
                left = mixed[:kept, side * width : (side + 1) * width]
                right = mixed[kept:, side * width : (side + 1) * width]
                product = lax.dot_general(
                    left, right, (((1,), (1,)), ((), ())), preferred_element_type=jnp.float32
                )
                wide[pl.ds(2 * pair + side, kept, stride=own), :] = product * (1.0 / width)
    for k in range(kept):
        out[:, pl.ds(k * kept, kept)] = wide[pl.ds(k * own, own), :].astype(jnp.bfloat16)
    area = send.at[pl.ds(0, len(ORDER) - 1)]
    pltpu.make_async_copy(area, area, send_sem).wait()


def shards(tables, indices, lengths, table_slot, dense_feature, left_proj, right_proj):
    tab_dev, samples, bag = indices.shape
    width = tables.shape[2]
    rows = tables.shape[1]
    own = dense_feature.shape[0]
    kept = left_proj.shape[0]
    count = table_slot.shape[0]
    devices = len(ORDER)
    table = np.zeros((8, devices * tab_dev), np.int32)
    for step, offset in enumerate(ORDER):
        for t in range(tab_dev):
            table[:5, step * tab_dev + t] = (*split_offset(offset), t)
    vmem = pl.BlockSpec(memory_space=pltpu.VMEM)
    return pl.pallas_call(
        kernel,
        out_shape=jax.ShapeDtypeStruct((own, kept * kept), jnp.bfloat16),
        in_specs=[vmem] * 8,
        out_specs=vmem,
        scratch_shapes=[
            pltpu.VMEM((tab_dev, width, rows), jnp.bfloat16),
            pltpu.VMEM((256 * tab_dev, width), jnp.float32),
            pltpu.VMEM((devices, own, tab_dev, width), jnp.bfloat16),
            pltpu.VMEM((own, devices * tab_dev, width), jnp.bfloat16),
            pltpu.VMEM((2 * kept, devices * tab_dev), jnp.bfloat16),
            pltpu.VMEM((count + 8, kept), jnp.float32),
            pltpu.VMEM((own // 2, 2 * kept, 2 * width), jnp.float32),
            pltpu.VMEM((kept * own, kept), jnp.float32),
            pltpu.SemaphoreType.DMA,
            pltpu.SemaphoreType.DMA((4,)),
            pltpu.SemaphoreType.REGULAR,
            pltpu.SemaphoreType.REGULAR,
            pltpu.SemaphoreType.REGULAR,
        ],
        compiler_params=pltpu.CompilerParams(
            collective_id=0, has_side_effects=True, vmem_limit_bytes=60 * 2**20
        ),
    )(
        tables,
        jnp.transpose(indices, (0, 2, 1)),
        lengths,
        table_slot.reshape(1, count),
        dense_feature,
        left_proj.T,
        right_proj.T,
        jnp.asarray(table),
    )


def solution(mesh):
    spread = P(AXES)
    return jax.shard_map(
        shards,
        mesh=mesh,
        in_specs=(spread, spread, spread, P(), spread, P(), P()),
        out_specs=spread,
        check_vma=False,
    )
```

time: 219 us -> 71.1 us (0.32); the launches traced: 215 us -> 70.9 us
  other arithmetic: 73.6 us -> 0 us
  Pallas kernels: 0 us -> 69 us
  waiting for transfers between devices: 53.3 us -> 0 us
  local copies, waits for them, and re-layouts: 48.8 us -> 1.87 us
  matrix products: 20.5 us -> 0 us
  starting transfers between devices: 11.9 us -> 0 us
  loops' own time: 7.05 us -> 0 us
    add x129 -> x0, other arithmetic: 72.8 us -> none  [the longest x128 72.8 us: add_ids(): return counts + hit.astype(jnp.bfloat16)]
    pallas_call x0 -> x1, Pallas kernels: none -> 69 us  [shards(): pl.pallas_call(kernel, out_shape=jax.ShapeDtypeStruct((own, kept * kept),...]
    all_to_all x1 -> x0, waiting for transfers between devices: 53.3 us -> none  [shards(): lax.all_to_all(blocks, ('hst', 'row', 'col'), split_axis=1, concat_axis=0...]
    dot_general x34 -> x0, matrix products: 20.5 us -> none  [the longest x32 15.7 us: one_block(): jnp.dot(counts, table, preferred_element_type=jnp.float32)]
    dynamic_slice x176 -> x0, local copies, waits for them, and re-layouts: 14.4 us -> none  [the longest x16 13 us: shards(): lax.map(lambda items: pool_table(items[0], items[1], items[2], bag_size),...]
    all_to_all x1 -> x0, starting transfers between devices: 11.9 us -> none  [shards(): lax.all_to_all(blocks, ('hst', 'row', 'col'), split_axis=1, concat_axis=0...]
    squeeze x40 -> x0, local copies, waits for them, and re-layouts: 8.11 us -> none  [the longest x8 7.79 us: shards(): lax.map(lambda items: pool_table(items[0], items[1], items[2], bag_size),...]
    another operation x41 -> x0, loops' own time: 7.05 us -> none  [the longest x32 5.09 us: one_block(): counts = lax.fori_loop(0, bag_size, add_ids, counts)]
  transfers between devices with their start and end apart: 1 -> 0, of which waited for: 1 -> 0; matrix products, arithmetic and copies ran while one was open for 0% -> 0% of each run, Pallas kernels for 0% -> 0%
where the time goes in v1:
time: 71.1 us; the launch traced here: 70.9 us
  Pallas kernels  69 us (97%)
  local copies, waits for them, and re-layouts  1.87 us (3%)
    pallas_call x1, Pallas kernels, shards(): pl.pallas_call(kernel, out_shape=jax.ShapeDtypeStruct((own, kept * kept),...  69 us
    unnamed x1, local copies, waits for them, and re-layouts  1.87 us

profile of v1, /device:TPU:1, one launch (start us, length us, event | category | flops | bytes accessed | tf_op | source)
XLA Modules:
  0.0 70.9 jit_solution(1242161182649947784)
XLA Ops:
  0.0 69.0 %shard_map.82 = bf16[16,16384]{1,0:T(8,128)(2,1)} custom-call(bf16[8,1024,128]{2,1,0:T(8,128)(2,1)} %tables.1, s32[8,4,2048]{2,1,0:T(4,128)} %bitcast.6, s32[8,2048]{1,0:T(8,128)} %lens.1, s32[1,1024]{1,0:T(1,128)} %bitcast.7, bf16[16,128]{1,0:T(8,128)(2,1)} %dense.1, bf16[1025,128]{1,0:T(8,128)(2,1)} %bitcast.4, bf16[1025,128]{1,0:T(8,128)(2,1)} %bitcast.5, ...), custom_call_target="tpu_custom_call" | custom-call | tf_op jit(solution)/shard_map/pallas_call | solution.py:203
  69.0 1.9 %copy.10 = bf16[16,16384]{1,0:T(8,128)(2,1)} copy(bf16[16,16384]{1,0:T(8,128)(2,1)} %shard_map.82) | data formatting | bytes 1048576

commit v2 on v1

--- a/solution.py
+++ b/solution.py
@@ -22,7 +22,14 @@
     return LINE[dx] + LINE[dz] + LINE[dy]
 
 
-ORDER = [0] + sorted(range(1, 128), key=lambda offset: -hops(offset))
+def far_first(offsets):
+    return sorted(offsets, key=lambda offset: -hops(offset))
+
+
+PLANE = far_first(range(1, 16))
+SLAB = far_first(range(16, 64))
+OTHER = far_first(range(64, 128))
+ORDER = [0] + PLANE + SLAB + OTHER
 
 
 def place():
@@ -45,15 +52,15 @@
 
 
 X_LINE = [(0, i, 0, 0) for i in (1, 2, 3)]
-Z_LINE = [(0, 0, i, 0) for i in (1, 2, 3)]
-Y_LINE = [(0, 0, 0, i) for i in (1, 2, 3)]
 H_LINE = [(1, 0, 0, 0)]
+FIRST = [split_offset(offset) for offset in PLANE] + X_LINE + H_LINE
 
 
 def kernel(
-    tables, ids, lens, slots, dense, left_t, right_t, steps, out,
+    tables_in, ids_in, lens_in, slots_in, dense_in, left_in, right_in, steps_in, out,
+    tables, ids, lens, slots, dense, left_t, right_t, steps,
     table_t, pooled, send, recv, proj, shifted, total, wide,
-    send_sem, recv_sem, x_sem, y_sem, h_sem,
+    load_sem, table_sem, send_sem, recv_sem, x_sem, h_sem,
 ):
     me = place()
     h, x, z, y = me
@@ -67,14 +74,39 @@
     depth = per_group * tab_dev
 
     barrier = pltpu.get_barrier_semaphore()
-    greet(me, barrier, X_LINE + Y_LINE + Z_LINE + H_LINE)
-
+    greet(me, barrier, FIRST)
+
+    def load(source, target, sem):
+        copy = pltpu.make_async_copy(source, target, sem)
+        copy.start()
+        return copy
+
+    early = [load(ids_in, ids, load_sem.at[0]), load(lens_in, lens, load_sem.at[1])]
+    parts = [load(tables_in.at[t], tables.at[t], table_sem.at[t]) for t in range(tab_dev)]
+    late = [
+        load(source, target, load_sem.at[2 + i])
+        for i, (source, target) in enumerate(
+            (
+                (slots_in, slots),
+                (dense_in, dense),
+                (left_in, left_t),
+                (right_in, right_t),
+                (steps_in, steps),
+            )
+        )
+    ]
     for t in range(tab_dev):
+        parts[t].wait()
         table_t[t] = tables[t].T
+    for copy in early:
+        copy.wait()
 
     iota = lax.broadcasted_iota(jnp.int32, (16, block), 0).astype(jnp.int16)
 
-    def pool_block(blk, _):
+    def pool_block(i, _):
+        turn = lax.rem(i, 4)
+        dx = lax.rem(turn * 2, 4) + turn // 2
+        blk = lax.rem(h + i // 4, 2) * 4 + lax.rem(x + dx, 4)
         start = pl.multiple_of(blk * block, block)
         for t in range(tab_dev):
             length = lens[pl.ds(t, 1), pl.ds(start, block)]
@@ -109,32 +141,33 @@
             send[blk * (block // own) + part] = piece.reshape(own, tab_dev, width).astype(jnp.bfloat16)
         return 0
 
-    blocks = samples // block
-    quarter = blocks // 4
-    lax.fori_loop(0, quarter, pool_block, 0)
-    pl.semaphore_wait(barrier, 10)
+    def post(first_step, steps_here):
+        for step in range(first_step, first_step + len(steps_here)):
+            to_h, to_x, to_c = partner(me, *split_offset(ORDER[step]))
+            pltpu.make_async_remote_copy(
+                src_ref=send.at[to_h * 64 + to_x * 16 + to_c],
+                dst_ref=recv.at[:, pl.ds(step * tab_dev, tab_dev), :],
+                send_sem=send_sem,
+                recv_sem=recv_sem.at[step // per_group],
+                device_id=(to_h, to_x, to_c),
+                device_id_type=MESH,
+            ).start()
+
+    lax.fori_loop(0, 3, pool_block, 0)
+    pl.semaphore_wait(barrier, len(FIRST))
     greet(me, x_sem, X_LINE)
-    lax.fori_loop(quarter, 2 * quarter, pool_block, 0)
-    pl.semaphore_wait(x_sem, 3)
-    greet(me, y_sem, Y_LINE)
-    lax.fori_loop(2 * quarter, 3 * quarter, pool_block, 0)
-    pl.semaphore_wait(y_sem, 3)
+    post(1, PLANE)
+    lax.fori_loop(3, 4, pool_block, 0)
+    pl.semaphore_wait(x_sem, len(X_LINE))
     greet(me, h_sem, H_LINE)
-    lax.fori_loop(3 * quarter, blocks, pool_block, 0)
-    pl.semaphore_wait(h_sem, 1)
-
-    for step in range(1, len(ORDER)):
-        to_h, to_x, to_c = partner(me, *split_offset(ORDER[step]))
-        pltpu.make_async_remote_copy(
-            src_ref=send.at[to_h * 64 + to_x * 16 + to_c],
-            dst_ref=recv.at[:, pl.ds(step * tab_dev, tab_dev), :],
-            send_sem=send_sem,
-            recv_sem=recv_sem.at[step // per_group],
-            device_id=(to_h, to_x, to_c),
-            device_id_type=MESH,
-        ).start()
+    post(16, SLAB)
+    lax.fori_loop(4, samples // block, pool_block, 0)
+    pl.semaphore_wait(h_sem, len(H_LINE))
+    post(64, OTHER)
     recv[:, 0:tab_dev, :] = send[h * 64 + x * 16 + z * 4 + y]
 
+    for copy in late:
+        copy.wait()
     kept = left_t.shape[1]
     from_h = lax.rem(h + 2 - steps[0:1, :], 2)
     from_x = lax.rem(x + 4 - steps[1:2, :], 4)
@@ -203,9 +236,17 @@
     return pl.pallas_call(
         kernel,
         out_shape=jax.ShapeDtypeStruct((own, kept * kept), jnp.bfloat16),
-        in_specs=[vmem] * 8,
+        in_specs=[pl.BlockSpec(memory_space=pltpu.HBM)] * 8,
         out_specs=vmem,
         scratch_shapes=[
+            pltpu.VMEM((tab_dev, rows, width), jnp.bfloat16),
+            pltpu.VMEM((tab_dev, bag, samples), jnp.int32),
+            pltpu.VMEM((tab_dev, samples), jnp.int32),
+            pltpu.VMEM((1, count), jnp.int32),
+            pltpu.VMEM((own, width), jnp.bfloat16),
+            pltpu.VMEM((count + 1, kept), jnp.bfloat16),
+            pltpu.VMEM((count + 1, kept), jnp.bfloat16),
+            pltpu.VMEM((8, devices * tab_dev), jnp.int32),
             pltpu.VMEM((tab_dev, width, rows), jnp.bfloat16),
             pltpu.VMEM((256 * tab_dev, width), jnp.float32),
             pltpu.VMEM((devices, own, tab_dev, width), jnp.bfloat16),
@@ -214,9 +255,10 @@
             pltpu.VMEM((count + 8, kept), jnp.float32),
             pltpu.VMEM((own // 2, 2 * kept, 2 * width), jnp.float32),
             pltpu.VMEM((kept * own, kept), jnp.float32),
+            pltpu.SemaphoreType.DMA((7,)),
+            pltpu.SemaphoreType.DMA((tab_dev,)),
             pltpu.SemaphoreType.DMA,
             pltpu.SemaphoreType.DMA((4,)),
-            pltpu.SemaphoreType.REGULAR,
             pltpu.SemaphoreType.REGULAR,
             pltpu.SemaphoreType.REGULAR,
         ],

time: 71.1 us -> 65.3 us (0.918)
  Pallas kernels: 69 us -> 63 us
    pallas_call x1, Pallas kernels: 69 us -> 63 us  [shards(): pl.pallas_call(kernel, out_shape=jax.ShapeDtypeStruct((own, kept * kept),...]
where the time goes in v2:
time: 65.3 us; the launch traced here: 64.9 us
  Pallas kernels  63 us (96%)
  local copies, waits for them, and re-layouts  1.87 us (3%)
    pallas_call x1, Pallas kernels, shards(): pl.pallas_call(kernel, out_shape=jax.ShapeDtypeStruct((own, kept * kept),...  63 us
    unnamed x1, local copies, waits for them, and re-layouts  1.87 us

profile of v2, /device:TPU:1, one launch (start us, length us, event | category | flops | bytes accessed | tf_op | source)
XLA Modules:
  0.0 64.9 jit_solution(12050292703406126850)
XLA Ops:
  0.0 63.0 %shard_map.82 = bf16[16,16384]{1,0:T(8,128)(2,1)} custom-call(bf16[8,1024,128]{2,1,0:T(8,128)(2,1)} %tables_in.1, s32[8,4,2048]{2,1,0:T(4,128)} %bitcast.6, s32[8,2048]{1,0:T(8,128)} %lens_in.1, s32[1,1024]{1,0:T(1,128)} %bitcast.7, bf16[16,128]{1,0:T(8,128)(2,1)} %dense_in.1, bf16[1025,128]{1,0:T(8,128)(2,1)} %bitcast.4, bf16[1025,128]{1,0:T(8,128)(2,1)} %bitcast.5, ...), custom_call_target="tpu_custom_call" | custom-call | tf_op jit(solution)/shard_map/pallas_call | solution.py:236
  63.0 1.9 %copy.10 = bf16[16,16384]{1,0:T(8,128)(2,1)} copy(bf16[16,16384]{1,0:T(8,128)(2,1)} %shard_map.82) | data formatting | bytes 1048576

commit v3 on v2

--- a/solution.py
+++ b/solution.py
@@ -27,7 +27,7 @@
 
 
 PLANE = far_first(range(1, 16))
-SLAB = far_first(range(16, 64))
+SLAB = far_first(range(32, 48)) + far_first([*range(16, 32), *range(48, 64)])
 OTHER = far_first(range(64, 128))
 ORDER = [0] + PLANE + SLAB + OTHER
 
@@ -95,20 +95,20 @@
             )
         )
     ]
-    for t in range(tab_dev):
-        parts[t].wait()
-        table_t[t] = tables[t].T
     for copy in early:
         copy.wait()
 
     iota = lax.broadcasted_iota(jnp.int32, (16, block), 0).astype(jnp.int16)
 
-    def pool_block(i, _):
+    def pool_block(i, _, first=False):
         turn = lax.rem(i, 4)
         dx = lax.rem(turn * 2, 4) + turn // 2
         blk = lax.rem(h + i // 4, 2) * 4 + lax.rem(x + dx, 4)
         start = pl.multiple_of(blk * block, block)
         for t in range(tab_dev):
+            if first:
+                parts[t].wait()
+                table_t[t] = tables[t].T
             length = lens[pl.ds(t, 1), pl.ds(start, block)]
             row_ids = []
             for j in range(bag):
@@ -153,15 +153,17 @@
                 device_id_type=MESH,
             ).start()
 
-    lax.fori_loop(0, 3, pool_block, 0)
+    pool_block(0, 0, first=True)
     pl.semaphore_wait(barrier, len(FIRST))
     greet(me, x_sem, X_LINE)
     post(1, PLANE)
-    lax.fori_loop(3, 4, pool_block, 0)
+    lax.fori_loop(1, 2, pool_block, 0)
     pl.semaphore_wait(x_sem, len(X_LINE))
     greet(me, h_sem, H_LINE)
-    post(16, SLAB)
-    lax.fori_loop(4, samples // block, pool_block, 0)
+    post(16, SLAB[:16])
+    lax.fori_loop(2, 4, pool_block, 0)
+    post(32, SLAB[16:])
+    lax.fori_loop(4, 8, pool_block, 0)
     pl.semaphore_wait(h_sem, len(H_LINE))
     post(64, OTHER)
     recv[:, 0:tab_dev, :] = send[h * 64 + x * 16 + z * 4 + y]

time: 65.3 us -> 64.7 us (level)
  no operation moved by 1% of the time
where the time goes in v3:
time: 64.7 us; the launch traced here: 64.5 us
  Pallas kernels  62.7 us (97%)
  local copies, waits for them, and re-layouts  1.87 us (3%)
    pallas_call x1, Pallas kernels, shards(): pl.pallas_call(kernel, out_shape=jax.ShapeDtypeStruct((own, kept * kept),...  62.7 us
    unnamed x1, local copies, waits for them, and re-layouts  1.87 us

profile of v3, /device:TPU:1, one launch (start us, length us, event | category | flops | bytes accessed | tf_op | source)
XLA Modules:
  0.0 64.5 jit_solution(17737520127886347565)
XLA Ops:
  0.0 62.7 %shard_map.82 = bf16[16,16384]{1,0:T(8,128)(2,1)} custom-call(bf16[8,1024,128]{2,1,0:T(8,128)(2,1)} %tables_in.1, s32[8,4,2048]{2,1,0:T(4,128)} %bitcast.6, s32[8,2048]{1,0:T(8,128)} %lens_in.1, s32[1,1024]{1,0:T(1,128)} %bitcast.7, bf16[16,128]{1,0:T(8,128)(2,1)} %dense_in.1, bf16[1025,128]{1,0:T(8,128)(2,1)} %bitcast.4, bf16[1025,128]{1,0:T(8,128)(2,1)} %bitcast.5, ...), custom_call_target="tpu_custom_call" | custom-call | tf_op jit(solution)/shard_map/pallas_call | solution.py:238
  62.7 1.9 %copy.10 = bf16[16,16384]{1,0:T(8,128)(2,1)} copy(bf16[16,16384]{1,0:T(8,128)(2,1)} %shard_map.82) | data formatting | bytes 1048576

commit v4 on v3

--- a/solution.py
+++ b/solution.py
@@ -10,25 +10,15 @@
 
 AXES = ("hst", "row", "col")
 MESH = pl.DeviceIdType.MESH
-LINE = (0, 1, 2, 1)
 
 
 def split_offset(offset):
     return offset // 64, offset // 16 % 4, offset // 4 % 4, offset % 4
 
 
-def hops(offset):
-    _, dx, dz, dy = split_offset(offset)
-    return LINE[dx] + LINE[dz] + LINE[dy]
-
-
-def far_first(offsets):
-    return sorted(offsets, key=lambda offset: -hops(offset))
-
-
-PLANE = far_first(range(1, 16))
-SLAB = far_first(range(32, 48)) + far_first([*range(16, 32), *range(48, 64)])
-OTHER = far_first(range(64, 128))
+PLANE = [10, 6, 9, 11, 14, 2, 5, 7, 8, 13, 15, 1, 3, 4, 12]
+SLAB = [42, 38, 41, 43, 46, 34, 37, 39, 40, 45, 47, 33, 35, 36, 44, 32, 26, 58, 22, 54, 25, 57, 27, 59, 30, 62, 18, 50, 21, 53, 23, 55, 24, 56, 29, 61, 31, 63, 17, 49, 19, 51, 20, 52, 28, 60, 16, 48]
+OTHER = [106, 102, 105, 90, 122, 107, 110, 98, 101, 86, 118, 103, 104, 89, 121, 74, 91, 123, 109, 85, 126, 111, 97, 82, 114, 99, 100, 94, 117, 70, 87, 119, 88, 120, 73, 75, 108, 93, 125, 78, 95, 127, 96, 81, 113, 66, 83, 115, 84, 116, 69, 71, 72, 92, 124, 77, 79, 80, 112, 65, 67, 68, 76, 64]
 ORDER = [0] + PLANE + SLAB + OTHER
 
 

time: 64.7 us -> 64.6 us (level)
  no operation moved by 1% of the time
where the time goes in v4:
time: 64.6 us; the launch traced here: 64.5 us
  Pallas kernels  62.6 us (97%)
  local copies, waits for them, and re-layouts  1.87 us (3%)
    pallas_call x1, Pallas kernels, shards(): pl.pallas_call(kernel, out_shape=jax.ShapeDtypeStruct((own, kept * kept),...  62.6 us
    unnamed x1, local copies, waits for them, and re-layouts  1.87 us

profile of v4, /device:TPU:1, one launch (start us, length us, event | category | flops | bytes accessed | tf_op | source)
XLA Modules:
  0.0 64.5 jit_solution(17345430231182155339)
XLA Ops:
  0.0 62.6 %shard_map.82 = bf16[16,16384]{1,0:T(8,128)(2,1)} custom-call(bf16[8,1024,128]{2,1,0:T(8,128)(2,1)} %tables_in.1, s32[8,4,2048]{2,1,0:T(4,128)} %bitcast.6, s32[8,2048]{1,0:T(8,128)} %lens_in.1, s32[1,1024]{1,0:T(1,128)} %bitcast.7, bf16[16,128]{1,0:T(8,128)(2,1)} %dense_in.1, bf16[1025,128]{1,0:T(8,128)(2,1)} %bitcast.4, bf16[1025,128]{1,0:T(8,128)(2,1)} %bitcast.5, ...), custom_call_target="tpu_custom_call" | custom-call | tf_op jit(solution)/shard_map/pallas_call | solution.py:228
  62.6 1.9 %copy.10 = bf16[16,16384]{1,0:T(8,128)(2,1)} copy(bf16[16,16384]{1,0:T(8,128)(2,1)} %shard_map.82) | data formatting | bytes 1048576

commit v5 on v4

--- a/solution.py
+++ b/solution.py
@@ -49,8 +49,8 @@
 def kernel(
     tables_in, ids_in, lens_in, slots_in, dense_in, left_in, right_in, steps_in, out,
     tables, ids, lens, slots, dense, left_t, right_t, steps,
-    table_t, pooled, send, recv, proj, shifted, total, wide,
-    load_sem, table_sem, send_sem, recv_sem, x_sem, h_sem,
+    table_t, pooled, send, recv, proj, shifted, total, wide, flat,
+    out_sem, load_sem, table_sem, send_sem, recv_sem, x_sem, h_sem,
 ):
     me = place()
     h, x, z, y = me
@@ -183,6 +183,7 @@
         row = dense[b : b + 1, :].astype(jnp.float32)
         total[b // 2, :, pl.ds(b % 2 * width, width)] = first * row
 
+    stores = []
     for group in range(groups):
         arrived = per_group - (1 if group == 0 else 0)
         area = send.at[pl.ds(0, arrived)]
@@ -206,10 +207,17 @@
                     left, right, (((1,), (1,)), ((), ())), preferred_element_type=jnp.float32
                 )
                 wide[pl.ds(2 * pair + side, kept, stride=own), :] = product * (1.0 / width)
-    for k in range(kept):
-        out[:, pl.ds(k * kept, kept)] = wide[pl.ds(k * own, own), :].astype(jnp.bfloat16)
+            if (2 * pair + 2) % 8 == 0:
+                low = 2 * pair - 6
+                for k in range(kept):
+                    flat[low // 8, :, pl.ds(k * kept, kept)] = wide[
+                        pl.ds(k * own + low, 8), :
+                    ].astype(jnp.bfloat16)
+                stores.append(load(flat.at[low // 8], out.at[pl.ds(low, 8), :], out_sem.at[low // 8]))
     area = send.at[pl.ds(0, len(ORDER) - 1)]
     pltpu.make_async_copy(area, area, send_sem).wait()
+    for copy in stores:
+        copy.wait()
 
 
 def shards(tables, indices, lengths, table_slot, dense_feature, left_proj, right_proj):
@@ -224,12 +232,11 @@
     for step, offset in enumerate(ORDER):
         for t in range(tab_dev):
             table[:5, step * tab_dev + t] = (*split_offset(offset), t)
-    vmem = pl.BlockSpec(memory_space=pltpu.VMEM)
     return pl.pallas_call(
         kernel,
         out_shape=jax.ShapeDtypeStruct((own, kept * kept), jnp.bfloat16),
         in_specs=[pl.BlockSpec(memory_space=pltpu.HBM)] * 8,
-        out_specs=vmem,
+        out_specs=pl.BlockSpec(memory_space=pltpu.HBM),
         scratch_shapes=[
             pltpu.VMEM((tab_dev, rows, width), jnp.bfloat16),
             pltpu.VMEM((tab_dev, bag, samples), jnp.int32),
@@ -247,6 +254,8 @@
             pltpu.VMEM((count + 8, kept), jnp.float32),
             pltpu.VMEM((own // 2, 2 * kept, 2 * width), jnp.float32),
             pltpu.VMEM((kept * own, kept), jnp.float32),
+            pltpu.VMEM((own // 8, 8, kept * kept), jnp.bfloat16),
+            pltpu.SemaphoreType.DMA((own // 8,)),
             pltpu.SemaphoreType.DMA((7,)),
             pltpu.SemaphoreType.DMA((tab_dev,)),
             pltpu.SemaphoreType.DMA,

time: 64.6 us -> 64.6 us (level)
  no operation moved by 1% of the time
where the time goes in v5:
time: 64.6 us; the launch traced here: 64.4 us
  Pallas kernels  62.5 us (97%)
  local copies, waits for them, and re-layouts  1.87 us (3%)
    pallas_call x1, Pallas kernels, shards(): pl.pallas_call(kernel, out_shape=jax.ShapeDtypeStruct((own, kept * kept),...  62.5 us
    unnamed x1, local copies, waits for them, and re-layouts  1.87 us

profile of v5, /device:TPU:1, one launch (start us, length us, event | category | flops | bytes accessed | tf_op | source)
XLA Modules:
  0.0 64.4 jit_solution(5273591705469514088)
XLA Ops:
  0.0 62.5 %shard_map.82 = bf16[16,16384]{1,0:T(8,128)(2,1)} custom-call(bf16[8,1024,128]{2,1,0:T(8,128)(2,1)} %tables_in.1, s32[8,4,2048]{2,1,0:T(4,128)} %bitcast.6, s32[8,2048]{1,0:T(8,128)} %lens_in.1, s32[1,1024]{1,0:T(1,128)} %bitcast.7, bf16[16,128]{1,0:T(8,128)(2,1)} %dense_in.1, bf16[1025,128]{1,0:T(8,128)(2,1)} %bitcast.4, bf16[1025,128]{1,0:T(8,128)(2,1)} %bitcast.5, ...), custom_call_target="tpu_custom_call" | custom-call | tf_op jit(solution)/shard_map/pallas_call | solution.py:235
  62.5 1.9 %copy.10 = bf16[16,16384]{1,0:T(8,128)(2,1)} copy(bf16[16,16384]{1,0:T(8,128)(2,1)} %shard_map.82) | data formatting | bytes 1048576
